TPU v7x, 32 devices: a whole 2x2x4 slice. The times are simulated.
32 devices in a mesh: rows: 8 (over z, x), cols: 4 (over y, core).
Axes of the slice: x: 2, y: 2, z: 4, core: 2. Of those that a mesh axis runs over, the one named last changes fastest.
Arguments:
- matrix: float32 [512, 32, 2, 128], P('rows', 'cols'), may hold values from -54 to 54
- plan: int32 [2, 4, 256], replicated, may hold values from 0 to 255, as said below
Outputs:
- rotated: float32 [512, 32, 2, 128], P('rows', 'cols')
Inputs may be any that keep to these rules, and one draw needn't show every extreme that they name: Each plan[s, r] pairs the 256 columns: partner of partner of i is i, and no column is its own partner.
All inputs are finite; a program needn't handle non-finite values.
Results may differ from a plain program's by a relative error of at most 0.0003.
Values sent between devices are 32-bit elements; how exact they have to be, the bound alone decides.
A program may use at most 128 MiB of HBM per device.

v0:
```python
import jax
import jax.numpy as jnp
from jax import lax
from jax.sharding import PartitionSpec as P

STEPS = 2


def passed_along(block, axis, distance):
    devices = range(lax.axis_size(axis))
    route = [((i - distance) % len(devices), i) for i in devices]
    return lax.ppermute(block, axis, route)


def diagonalize(grams, table):
    width = grams.shape[1]
    indices = jnp.arange(width, dtype=jnp.int32)
    rotation = jnp.broadcast_to(jnp.eye(width, dtype=jnp.float32), grams.shape)
    unit_matrix = jnp.eye(width, dtype=jnp.float32)
    for round_index in range(table.shape[0]):
        partner = table[round_index]
        onehot = (partner[:, None] == indices[None, :]).astype(jnp.float32)
        diagonal_now = jnp.diagonal(grams, axis1=1, axis2=2)
        partner_diag = jnp.einsum(
            "pj,ij->pi", diagonal_now, onehot, precision=lax.Precision.HIGHEST
        )
        partner_gram = jnp.sum(grams * onehot[None], axis=2)
        orient = jnp.where(indices < partner, 1.0, -1.0).astype(jnp.float32)
        spread = orient[None, :] * (partner_diag - diagonal_now)
        sign_part = jnp.where(spread >= 0.0, 1.0, -1.0).astype(jnp.float32)
        tangent = (
            sign_part
            * 2.0
            * partner_gram
            / (jnp.abs(spread) + jnp.sqrt(spread * spread + 4.0 * partner_gram * partner_gram))
        )
        cosine = 1.0 / jnp.sqrt(1.0 + tangent * tangent)
        sine_part = tangent * cosine
        off_part = jnp.swapaxes(onehot[None] * (-orient[None, :] * sine_part)[:, :, None], 1, 2)
        rot_now = cosine[:, :, None] * unit_matrix[None] + off_part
        product = jnp.einsum("pij,pjk->pik", grams, rot_now, precision=lax.Precision.HIGHEST)
        grams = jnp.einsum("pji,pjk->pik", rot_now, product, precision=lax.Precision.HIGHEST)
        rotation = jnp.einsum("pij,pjk->pik", rotation, rot_now, precision=lax.Precision.HIGHEST)
    return (grams, rotation)


def full_grams(columns):
    local_sum = jnp.einsum("mpi,mpj->pij", columns, columns, precision=lax.Precision.HIGHEST)
    return lax.psum(local_sum, "rows")


def body(matrix, plan):
    rows_here, pair_here, halves, width = matrix.shape
    columns = matrix.reshape(rows_here, pair_here, halves * width)
    grams = full_grams(columns)
    for step_index in range(STEPS):
        grams, rotation = diagonalize(grams, plan[step_index])
        columns = jnp.einsum("mpi,pij->mpj", columns, rotation, precision=lax.Precision.HIGHEST)
        quarter = columns.reshape(rows_here, pair_here, halves, width)
        tops = quarter[:, :, 0, :]
        bottoms = quarter[:, :, 1, :]
        bottoms, low_grams = passed_along((bottoms, grams[:, width:, width:]), "cols", 1)
        columns = jnp.stack([tops, bottoms], axis=2).reshape(rows_here, pair_here, halves * width)
        if step_index + 1 < STEPS:
            cross_local = jnp.einsum("mpi,mpj->pij", tops, bottoms, precision=lax.Precision.HIGHEST)
            cross = lax.psum(cross_local, "rows")
            upper_rows = jnp.concatenate([grams[:, :width, :width], cross], axis=2)
            lower_rows = jnp.concatenate([jnp.swapaxes(cross, 1, 2), low_grams], axis=2)
            grams = jnp.concatenate([upper_rows, lower_rows], axis=1)
    return columns.reshape(matrix.shape)


def solution(mesh):
    in_specs = (P("rows", "cols", None, None), P())
    out_specs = P("rows", "cols", None, None)
    return jax.shard_map(body, mesh=mesh, in_specs=in_specs, out_specs=out_specs, check_vma=False)
```

profile of v0, /device:TPU:0, one launch (start us, length us, event | category | flops | bytes accessed | tf_op | source)
XLA Modules:
  0.0 463.2 jit_solution(2592383849989567668)
XLA Ops:
  6.5 1.5 reshape.364
  8.0 3.2 fusion.123
  14.9 0.7 fusion.136
  22.8 0.7 fusion.125
  23.5 0.9 fusion.134
  24.4 92.0 %all-reduce.3.cloned.1.call-done = f32[8,256,256]{2,1,0:T(8,128)} async-done(((f32[8,256,256]{2,1,0:T(8,128)}), f32[8,256,256]{2,1,0:T(8,128)}) %all-reduce.3.cloned.1.call-update) | async-done | bytes 2097168 | tf_op jit(solution)/shard_map/psum | solution.py:49
  116.4 17.5 %copy.30 = f32[8,256,256]{0,2,1:T(8,128)} copy(f32[8,256,256]{2,1,0:T(8,128)} %all-reduce.3.cloned.1.call-done) | data formatting | bytes 4194304 | tf_op jit(solution)/shard_map/psum | solution.py:49
  133.9 2.3 gather_fusion
  136.3 1.4 multiply_reduce_fusion.7
  137.7 1.0 add_rsqrt_fusion.7
  138.7 3.5 fusion.22
  142.2 4.1 fusion.24
  146.3 3.3 multiply_reduce_fusion.6
  149.6 16.5 %copy.32 = f32[8,256,256]{0,2,1:T(8,128)} copy(f32[8,256,256]{1,2,0:T(8,128)S(1)} %get-tuple-element.56) | data formatting | bytes 4194304 | tf_op jit(solution)/shard_map/pji,pjk->pik/dot_general | solution.py:42
  166.1 2.3 gather_fusion.1
  169.1 1.0 add_rsqrt_fusion.6
  170.1 5.1 %fusion.21 = f32[8,256,256]{1,2,0:T(8,128)S(1)} fusion(f32[8,256,256]{1,2,0:T(8,128)S(1)} %get-tuple-element.56, f32[8,256]{1,0:T(8,128)S(1)} %get-tuple-element.34, f32[256,256]{1,0:T(8,128)} %fusion.135, f32[8,256]{1,0:T(8,128)S(1)} %get-tuple-element.33, f32[256,256]{1,0:T(8,128)S(1)} %get-tuple-element.67), kind=kOutput, calls=%fused_computation.42 | convolution fusion | flops 1612185600 | bytes 4734976 | tf_op jit(solution)/shard_map/pij,pjk->pik/dot_general | solution.py:41
  175.2 3.3 multiply_reduce_fusion.5
  178.6 16.6 %copy.34 = f32[8,256,256]{0,2,1:T(8,128)} copy(f32[8,256,256]{1,2,0:T(8,128)S(1)} %get-tuple-element.58) | data formatting | bytes 4194304 | tf_op jit(solution)/shard_map/pji,pjk->pik/dot_general | solution.py:42
  195.2 2.3 gather_fusion.2
  198.2 1.0 add_rsqrt_fusion.5
  199.3 5.1 %fusion.18 = f32[8,256,256]{1,2,0:T(8,128)S(1)} fusion(f32[8,256,256]{1,2,0:T(8,128)S(1)} %get-tuple-element.58, f32[8,256]{1,0:T(8,128)S(1)} %get-tuple-element.32, f32[256,256]{1,0:T(8,128)} %fusion.136, f32[8,256]{1,0:T(8,128)S(1)} %get-tuple-element.31, f32[256,256]{1,0:T(8,128)S(1)} %get-tuple-element.67), kind=kOutput, calls=%fused_computation.37 | convolution fusion | flops 1612185600 | bytes 4734976 | tf_op jit(solution)/shard_map/pij,pjk->pik/dot_general | solution.py:41
  204.4 3.3 multiply_reduce_fusion.4
  207.8 16.4 %copy.36 = f32[8,256,256]{0,2,1:T(8,128)} copy(f32[8,256,256]{1,2,0:T(8,128)S(1)} %get-tuple-element.60) | data formatting | bytes 4194304 | tf_op jit(solution)/shard_map/pji,pjk->pik/dot_general | solution.py:42
  224.2 2.3 gather_fusion.3
  227.2 1.0 add_rsqrt_fusion.4
  228.2 5.1 %fusion.15 = f32[8,256,256]{1,2,0:T(8,128)S(1)} fusion(f32[8,256,256]{1,2,0:T(8,128)S(1)} %get-tuple-element.60, f32[8,256]{1,0:T(8,128)S(1)} %get-tuple-element.30, f32[256,256]{1,0:T(8,128)} %fusion.137, f32[8,256]{1,0:T(8,128)S(1)} %get-tuple-element.29, f32[256,256]{1,0:T(8,128)S(1)} %get-tuple-element.67), kind=kOutput, calls=%fused_computation.32 | convolution fusion | flops 1612185600 | bytes 4734976 | tf_op jit(solution)/shard_map/pij,pjk->pik/dot_general | solution.py:41
  233.3 2.6 fusion.14
  236.0 2.5 fusion.19
  238.5 2.7 fusion.16
  241.3 2.5 fusion.13
  243.8 2.4 convolution_bitcast_fusion.1
  246.2 2.1 reshape.365
  248.3 1.7 fusion.192
  250.1 1.1 fusion.190
  251.1 1.6 collective-permute-start.1
  252.7 3.1 collective-permute-done
  255.8 1.8 fusion.194
  258.5 1.1 copy.70
  259.6 70.2 %all-reduce.5.cloned.1.call-done = f32[8,128,128]{1,2,0:T(8,128)} async-done(((f32[8,128,128]{1,2,0:T(8,128)}), f32[8,128,128]{1,2,0:T(8,128)}) %all-reduce.5.cloned.1.call-update) | async-done | bytes 524304 | tf_op jit(solution)/shard_map/psum | solution.py:66
  329.8 1.2 copy.42
  331.0 0.8 copy-done.23
  331.9 1.7 maximum_maximum_fusion
  333.6 16.7 %copy.43 = f32[8,256,256]{0,2,1:T(8,128)} copy(f32[8,256,256]{1,2,0:T(8,128)S(1)} %get-tuple-element.5) | data formatting | bytes 4194304 | tf_op jit(solution)/shard_map/concatenate | solution.py:69
  350.3 2.4 gather_fusion.4
  353.1 3.5 fusion.12
  356.6 4.1 fusion.11
  360.7 2.7 multiply_reduce_fusion.2
  363.5 16.4 %copy.45 = f32[8,256,256]{0,2,1:T(8,128)} copy(f32[8,256,256]{1,2,0:T(8,128)S(1)} %get-tuple-element.62) | data formatting | bytes 4194304 | tf_op jit(solution)/shard_map/pji,pjk->pik/dot_general | solution.py:42
  380.0 2.3 gather_fusion.5
  382.6 4.1 fusion.8
  386.8 3.8 fusion.9
  390.5 2.7 multiply_reduce_fusion.1
  393.3 16.5 %copy.47 = f32[8,256,256]{0,2,1:T(8,128)} copy(f32[8,256,256]{1,2,0:T(8,128)S(1)} %get-tuple-element.64) | data formatting | bytes 4194304 | tf_op jit(solution)/shard_map/pji,pjk->pik/dot_general | solution.py:42
  409.8 2.3 gather_fusion.6
  412.5 4.1 fusion.5
  416.6 3.8 fusion.6
  420.4 2.7 multiply_reduce_fusion
  423.1 16.5 %copy.49 = f32[8,256,256]{0,2,1:T(8,128)} copy(f32[8,256,256]{1,2,0:T(8,128)S(1)} %get-tuple-element.66) | data formatting | bytes 4194304 | tf_op jit(solution)/shard_map/pji,pjk->pik/dot_general | solution.py:42
  439.6 2.3 gather_fusion.7
  442.3 4.1 fusion
  446.5 1.6 convolution_bitcast_fusion
  449.0 5.8 %collective-permute-done.2 = f32[64,8,128]{2,1,0:T(8,128)S(1)} collective-permute-done((f32[64,8,128]{2,1,0:T(8,128)S(1)}, f32[64,8,128]{2,1,0:T(8,128)S(1)}, u32[]{:S(2)}, u32[]{:S(2)}) %collective-permute-start.2) | collective-permute-done | bytes 262176 | tf_op jit(solution)/shard_map/ppermute | solution.py:12
  454.8 1.3 pad_maximum_fusion.1
  (140 shorter events, 16.1 us)
Async XLA Ops:
  6.5 109.9 %all-reduce.3.cloned.1.call-start = ((), (), s32[]{:S(2)}) async-start(), calls=%async_computation | async-start | bytes 4194304 | tf_op jit(solution)/shard_map/psum | solution.py:49
  8.0 3.5 copy-start.41
  11.2 318.5 %all-reduce.5.cloned.1.call-start = ((), (), s32[]{:S(2)}) async-start(), calls=%async_computation.1 | async-start | bytes 1048576 | tf_op jit(solution)/shard_map/psum | solution.py:66
  11.5 12.9 %copy-start.31 = (s32[1,1,256]{2,1,0:T(1,128)}, s32[1,1,256]{2,1,0:T(1,128)S(1)}, u32[]{:S(2)}) copy-start(s32[1,1,256]{2,1,0:T(1,128)S(1)} %get-tuple-element.22) | copy-start | bytes 3076
  11.5 12.9 %copy-start.33 = (s32[1,1,256]{2,1,0:T(1,128)}, s32[1,1,256]{2,1,0:T(1,128)S(1)}, u32[]{:S(2)}) copy-start(s32[1,1,256]{2,1,0:T(1,128)S(1)} %get-tuple-element.16) | copy-start | bytes 3076
  11.5 12.9 %copy-start.35 = (s32[1,1,256]{2,1,0:T(1,128)}, s32[1,1,256]{2,1,0:T(1,128)S(1)}, u32[]{:S(2)}) copy-start(s32[1,1,256]{2,1,0:T(1,128)S(1)} %get-tuple-element.21) | copy-start | bytes 3076
  11.5 12.9 %copy-start.37 = (s32[1,1,256]{2,1,0:T(1,128)}, s32[1,1,256]{2,1,0:T(1,128)S(1)}, u32[]{:S(2)}) copy-start(s32[1,1,256]{2,1,0:T(1,128)S(1)} %get-tuple-element.20) | copy-start | bytes 3076
  11.5 12.9 %copy-start.38 = (s32[1,1,256]{2,1,0:T(1,128)}, s32[1,1,256]{2,1,0:T(1,128)S(1)}, u32[]{:S(2)}) copy-start(s32[1,1,256]{2,1,0:T(1,128)S(1)} %get-tuple-element.19) | copy-start | bytes 3076
  11.5 12.9 %copy-start.39 = (s32[1,1,256]{2,1,0:T(1,128)}, s32[1,1,256]{2,1,0:T(1,128)S(1)}, u32[]{:S(2)}) copy-start(s32[1,1,256]{2,1,0:T(1,128)S(1)} %get-tuple-element.18) | copy-start | bytes 3076
  11.6 12.9 %copy-start.40 = (s32[1,1,256]{2,1,0:T(1,128)}, s32[1,1,256]{2,1,0:T(1,128)S(1)}, u32[]{:S(2)}) copy-start(s32[1,1,256]{2,1,0:T(1,128)S(1)} %get-tuple-element.17) | copy-start | bytes 3076
  116.4 19.9 %copy-start = (f32[8,256,256]{2,1,0:T(8,128)S(1)}, f32[8,256,256]{2,1,0:T(8,128)}, u32[]{:S(2)}) copy-start(f32[8,256,256]{2,1,0:T(8,128)} %all-reduce.3.cloned.1.call-done) | copy-start | bytes 6291460
  136.3 2.4 copy-start.9
  142.2 4.1 copy-start.22
  170.1 5.1 %copy-start.25 = (f32[8,256]{1,0:T(8,128)}, f32[8,256]{1,0:T(8,128)S(1)}, u32[]{:S(2)}) copy-start(f32[8,256]{1,0:T(8,128)S(1)} %get-tuple-element.34) | copy-start | bytes 24580
  170.1 5.1 %copy-start.4 = (f32[256,256]{1,0:T(8,128)S(1)}, f32[256,256]{1,0:T(8,128)}, u32[]{:S(2)}) copy-start(f32[256,256]{1,0:T(8,128)} %fusion.135) | copy-start | bytes 786436
  170.1 5.1 %copy-start.21 = (f32[256,256]{0,1:T(8,128)S(1)}, f32[256,256]{0,1:T(8,128)}, u32[]{:S(2)}) copy-start(f32[256,256]{0,1:T(8,128)} %fusion.130) | copy-start | bytes 786436
  199.2 5.2 %copy-start.27 = (f32[8,256]{1,0:T(8,128)}, f32[8,256]{1,0:T(8,128)S(1)}, u32[]{:S(2)}) copy-start(f32[8,256]{1,0:T(8,128)S(1)} %get-tuple-element.31) | copy-start | bytes 24580
  199.2 5.2 %copy-start.29 = (f32[8,256]{1,0:T(8,128)}, f32[8,256]{1,0:T(8,128)S(1)}, u32[]{:S(2)}) copy-start(f32[8,256]{1,0:T(8,128)S(1)} %get-tuple-element.32) | copy-start | bytes 24580
  199.2 5.2 %copy-start.6 = (f32[256,256]{1,0:T(8,128)S(1)}, f32[256,256]{1,0:T(8,128)}, u32[]{:S(2)}) copy-start(f32[256,256]{1,0:T(8,128)} %fusion.136) | copy-start | bytes 786436
  199.3 5.2 %copy-start.20 = (f32[256,256]{0,1:T(8,128)S(1)}, f32[256,256]{0,1:T(8,128)}, u32[]{:S(2)}) copy-start(f32[256,256]{0,1:T(8,128)} %fusion.129) | copy-start | bytes 786436
  228.2 5.1 %copy-start.8 = (f32[256,256]{1,0:T(8,128)S(1)}, f32[256,256]{1,0:T(8,128)}, u32[]{:S(2)}) copy-start(f32[256,256]{1,0:T(8,128)} %fusion.137) | copy-start | bytes 786436
  233.3 2.6 copy-start.1
  233.3 2.6 copy-start.5
  233.3 2.6 copy-start.26
  236.0 2.5 copy-start.7
  236.0 2.5 copy-start.28
  236.0 2.5 copy-start.30
  250.0 5.8 %collective-permute-start = (f32[64,8,128]{2,0,1:T(8,128)S(1)}, f32[64,8,128]{2,0,1:T(8,128)S(1)}, u32[]{:S(2)}, u32[]{:S(2)}) collective-permute-start(f32[64,8,128]{2,0,1:T(8,128)S(1)} %bitcast.109), channel_id=1, source_target_pairs={{3,0},{0,1},{1,2},{2,3},{7,4},{4,5},{5,6},{6,7},{11,8},{8,9},{9,10... | collective-permute-start | bytes 786440 | tf_op jit(solution)/shard_map/ppermute | solution.py:12
  251.1 79.9 %collective-permute-start.1 = (f32[8,128,128]{1,2,0:T(8,128)}, f32[8,128,128]{1,2,0:T(8,128)S(1)}, u32[]{:S(2)}, u32[]{:S(2)}) collective-permute-start(f32[8,128,128]{1,2,0:T(8,128)} %get-tuple-element.8), channel_id=1, source_target_pairs={{3,0},{0,1},{1,2},{2,3},{7,4},{4,5},{5,6},{6,7},{11,8},{8,9},{9,10... | collective-permute-start | bytes 1572872 | tf_op jit(solution)/shard_map/ppermute | solution.py:12
  331.0 2.6 copy-start.12
  331.0 0.8 copy-start.23
  333.6 19.2 %copy-start.36 = (s32[1,1,256]{2,1,0:T(1,128)S(1)}, s32[1,1,256]{2,1,0:T(1,128)}, u32[]{:S(2)}) copy-start(s32[1,1,256]{2,1,0:T(1,128)} %copy-done.35) | copy-start | bytes 3076
  333.6 19.2 %copy-start.46 = (f32[256]{0:T(256)S(1)}, f32[256]{0:T(256)}, u32[]{:S(2)}) copy-start(f32[256]{0:T(256)} %get-tuple-element.43) | copy-start | bytes 3076
  333.6 19.2 %copy-start.47 = (f32[256]{0:T(256)S(1)}, f32[256]{0:T(256)}, u32[]{:S(2)}) copy-start(f32[256]{0:T(256)} %get-tuple-element.44) | copy-start | bytes 3076
  333.6 19.5 %copy-start.10 = (f32[256,256]{1,0:T(8,128)S(1)}, f32[256,256]{1,0:T(8,128)}, u32[]{:S(2)}) copy-start(f32[256,256]{1,0:T(8,128)} %fusion.138) | copy-start | bytes 786436
  350.3 6.2 %copy-start.11 = (f32[8,128,128]{1,2,0:T(8,128)S(1)}, f32[8,128,128]{1,2,0:T(8,128)}, u32[]{:S(2)}) copy-start(f32[8,128,128]{1,2,0:T(8,128)} %all-reduce.5.cloned.1.call-done) | copy-start | bytes 1572868
  350.3 6.2 %copy-start.13 = (f32[8,128,128]{1,2,0:T(8,128)S(1)}, f32[8,128,128]{1,2,0:T(8,128)}, u32[]{:S(2)}) copy-start(f32[8,128,128]{1,2,0:T(8,128)} %copy-done.12) | copy-start | bytes 1572868
  350.3 6.2 %copy-start.14 = (f32[8,128,128]{1,2,0:T(8,128)S(1)}, f32[8,128,128]{1,2,0:T(8,128)}, u32[]{:S(2)}) copy-start(f32[8,128,128]{1,2,0:T(8,128)} %get-tuple-element.7) | copy-start | bytes 1572868
  350.3 6.2 %copy-start.24 = (f32[8,128,128]{1,2,0:T(8,128)S(1)}, f32[8,128,128]{1,2,0:T(8,128)}, u32[]{:S(2)}) copy-start(f32[8,128,128]{1,2,0:T(8,128)} %copy-done.23) | copy-start | bytes 1572868
  356.6 4.1 copy-start.18
  363.5 18.9 %copy-start.34 = (s32[1,1,256]{2,1,0:T(1,128)S(1)}, s32[1,1,256]{2,1,0:T(1,128)}, u32[]{:S(2)}) copy-start(s32[1,1,256]{2,1,0:T(1,128)} %copy-done.33) | copy-start | bytes 3076
  363.5 18.9 %copy-start.44 = (f32[256]{0:T(256)S(1)}, f32[256]{0:T(256)}, u32[]{:S(2)}) copy-start(f32[256]{0:T(256)} %get-tuple-element.41) | copy-start | bytes 3076
  363.5 18.8 %copy-start.45 = (f32[256]{0:T(256)S(1)}, f32[256]{0:T(256)}, u32[]{:S(2)}) copy-start(f32[256]{0:T(256)} %get-tuple-element.42) | copy-start | bytes 3076
  382.6 4.1 copy-start.2
  386.8 3.8 copy-start.17
  393.3 18.9 %copy-start.32 = (s32[1,1,256]{2,1,0:T(1,128)S(1)}, s32[1,1,256]{2,1,0:T(1,128)}, u32[]{:S(2)}) copy-start(s32[1,1,256]{2,1,0:T(1,128)} %copy-done.31) | copy-start | bytes 3076
  393.3 18.9 %copy-start.42 = (f32[256]{0:T(256)S(1)}, f32[256]{0:T(256)}, u32[]{:S(2)}) copy-start(f32[256]{0:T(256)} %get-tuple-element.39) | copy-start | bytes 3076
  393.3 18.9 %copy-start.43 = (f32[256]{0:T(256)S(1)}, f32[256]{0:T(256)}, u32[]{:S(2)}) copy-start(f32[256]{0:T(256)} %get-tuple-element.40) | copy-start | bytes 3076
  412.5 4.1 copy-start.3
  416.6 3.8 copy-start.16
  423.1 19.2 %copy-start.19 = (f32[256,256]{1,0:T(8,128)S(1)}, f32[256,256]{1,0:T(8,128)}, u32[]{:S(2)}) copy-start(f32[256,256]{1,0:T(8,128)} %fusion.141) | copy-start | bytes 786436
  442.3 4.2 copy-start.15
  449.0 5.8 %collective-permute-start.2 = (f32[64,8,128]{2,1,0:T(8,128)S(1)}, f32[64,8,128]{2,1,0:T(8,128)S(1)}, u32[]{:S(2)}, u32[]{:S(2)}) collective-permute-start(f32[64,8,128]{2,1,0:T(8,128)S(1)} %bitcast.108), channel_id=1, source_target_pairs={{3,0},{0,1},{1,2},{2,3},{7,4},{4,5},{5,6},{6,7},{11,8},{8,9},{9,10... | collective-permute-start | bytes 786440 | tf_op jit(solution)/shard_map/ppermute | solution.py:12
Sparse Core Ops, SparseCore 0:
  11.4 105.0 all-reduce.2
  257.8 71.9 all-reduce.4
where the time goes:
time: 467 us; the launch traced here: 463 us
  waiting for transfers between devices  171 us (37%)
  local copies, waits for them, and re-layouts  165 us (35%)
  matrix products  92.9 us (20%)
  other arithmetic  18 us (4%)
  between operations  14.6 us (3%)
    dot_general x6, local copies, waits for them, and re-layouts, diagonalize(): jnp.einsum('pji,pjk->pik', rot_now, product, precision=lax.Precision.HIGH...  98.9 us
    psum x1, waiting for transfers between devices, full_grams(): return lax.psum(local_sum, 'rows')  92 us
    psum x1, waiting for transfers between devices, body(): cross = lax.psum(cross_local, 'rows')  70.2 us
    dot_general x7, matrix products, diagonalize(): jnp.einsum('pij,pjk->pik', grams, rot_now, precision=lax.Precision.HIGHEST)  31.7 us
    dot_general x8, matrix products, diagonalize(): jnp.einsum('pij,pjk->pik', rotation, rot_now, precision=lax.Precision.HIG...  26.3 us
    gather x16, local copies, waits for them, and re-layouts, diagonalize(): diagonal_now = jnp.diagonal(grams, axis1=1, axis2=2)  21 us
    dot_general x7, matrix products, diagonalize(): jnp.einsum('pji,pjk->pik', rot_now, product, precision=lax.Precision.HIGH...  20.8 us
    psum x1, local copies, waits for them, and re-layouts, full_grams(): return lax.psum(local_sum, 'rows')  17.5 us
  transfers between devices with their start and end apart: 5, of which 4 were waited for; matrix products, arithmetic and copies ran while one was open for 4% of the time, Pallas kernels for 0%

commit v1 on v0

v1 whole, which is shorter than its diff:
```python
import functools

import jax
import jax.numpy as jnp
from jax import lax
from jax.experimental import pallas as pl
from jax.experimental.pallas import tpu as pltpu
from jax.sharding import PartitionSpec as P

MESH = pl.DeviceIdType.MESH
NN = (((1,), (0,)), ((), ()))
NT = (((1,), (1,)), ((), ()))
F32 = jnp.float32
BF16 = jnp.bfloat16


def dot(a, b, dims=NN, precision=None):
    return lax.dot_general(a, b, dims, precision=precision, preferred_element_type=F32)


def exact_dot(a, b, dims=NN):
    return dot(a, b, dims, lax.Precision.HIGHEST)


def split(a):
    hi = a.astype(BF16)
    rest = a - hi.astype(F32)
    mid = rest.astype(BF16)
    lo = (rest - mid.astype(F32)).astype(BF16)
    return hi, mid, lo


def moved_columns(a, onehot):
    hi, mid, lo = split(a)
    return dot(hi, onehot) + dot(mid, onehot) + dot(lo, onehot)


def moved_transposed(a, onehot_t):
    hi, mid, lo = split(a)
    return dot(onehot_t, hi, NT) + dot(onehot_t, mid, NT) + dot(onehot_t, lo, NT)


def rotated_columns(a, cosine, sine):
    half = a.shape[1] // 2
    left, right = a[:, :half], a[:, half:]
    return jnp.concatenate([cosine * left - sine * right, sine * left + cosine * right], axis=1)


def angles(gram):
    half = gram.shape[0] // 2
    shape = (half, half)
    eye = lax.broadcasted_iota(jnp.int32, shape, 0) == lax.broadcasted_iota(jnp.int32, shape, 1)

    def diagonal(block):
        return jnp.sum(jnp.where(eye, block, 0.0), axis=0, keepdims=True)

    low = diagonal(gram[:half, :half])
    high = diagonal(gram[half:, half:])
    cross = diagonal(gram[:half, half:])
    spread = high - low
    sign = jnp.where(spread >= 0.0, 1.0, -1.0)
    root = jnp.sqrt(spread * spread + 4.0 * cross * cross)
    tangent = sign * 2.0 * cross / (jnp.abs(spread) + root)
    cosine = 1.0 / jnp.sqrt(1.0 + tangent * tangent)
    return cosine, tangent * cosine


def orders(partner):
    width = partner.shape[1]
    shape = (width, width)
    row = lax.broadcasted_iota(jnp.int32, shape, 0)
    col = lax.broadcasted_iota(jnp.int32, shape, 1)
    other = jnp.broadcast_to(partner, shape)
    swap = row == other
    one = jnp.ones(shape, BF16)

    def bits(mask):
        return jnp.where(mask, 1.0, 0.0).astype(BF16)

    swap_b = bits(swap)
    first_row = other > col
    rank_row = dot(bits(first_row), bits(row < col))
    mate_row = dot(rank_row.astype(BF16), swap_b)
    place_row = jnp.where(first_row, rank_row, mate_row + float(width // 2))
    first_col = dot(bits(swap & (col > row)), one) > 0.5
    rank_col = dot(bits(col < row), bits(first_col))
    mate_col = dot(swap_b, rank_col.astype(BF16))
    place_col = jnp.where(first_col, rank_col, mate_col + float(width // 2))
    forward = bits(place_col == col.astype(F32))
    backward = bits(place_row == row.astype(F32))
    return forward, backward


def diagonalizer(gram, step, moves, moves_t, rounds):
    rotation = None
    cosine = sine = None
    for r in range(rounds):
        move = moves[step, r]
        if r == 0:
            turned = moved_transposed(gram, moves_t[step, r])
            gram = moved_columns(turned, move)
            rotation = move.astype(F32)
        else:
            turned = moved_transposed(rotated_columns(gram, cosine, sine), moves_t[step, r])
            gram = moved_columns(rotated_columns(turned, cosine, sine), move)
            rotation = moved_columns(rotation, move)
        cosine, sine = angles(gram)
        rotation = rotated_columns(rotation, cosine, sine)
    return moved_columns(rotation, moves[step, rounds])


def kernel(sizes, x_ref, plan_ref, out_ref, stage, held, bottoms, landed, ytop, ybot, arrived, moves, moves_t, grams,
           in_send, in_recv, mid_sem, gram_send, gram_recv, top_send, top_recv, low_send, low_recv):
    owners, groups, cols, rows_here, steps, rounds, width = sizes
    half = width // 2
    rows_all = owners * rows_here
    me = lax.axis_index("rows")
    col = lax.axis_index("cols")
    group, mine = me // owners, me % owners
    right = (col + 1) % cols

    def at(owner_shift, col_shift=0, group_shift=0):
        row = ((group + group_shift) % groups) * owners + (mine + owner_shift) % owners
        return row, (col + col_shift) % cols

    peers = {(o, c, 0) for o in range(owners) for c in (0, 1, cols - 1)} | {(0, 0, g) for g in range(groups)}
    peers = sorted(peers - {(0, 0, 0)})
    barrier = pltpu.get_barrier_semaphore()
    for peer in peers:
        pl.semaphore_signal(barrier, inc=1, device_id=at(*peer), device_id_type=MESH)
    for k in range(owners):
        for h in range(2):
            stage[k, :, h * half:(h + 1) * half] = x_ref[pl.ds(2 * k + h, rows_here, stride=2 * owners), :]
    pl.semaphore_wait(barrier, len(peers))

    def rows_of(owner):
        return pl.ds(pl.multiple_of(owner * rows_here, rows_here), rows_here)

    incoming = []
    for d in range(1, owners):
        copy = pltpu.make_async_remote_copy(
            stage.at[(mine + d) % owners], held.at[rows_of(mine), :], in_send.at[d], in_recv.at[d],
            device_id=at(d), device_id_type=MESH)
        copy.start()
        incoming.append(copy)
    held[rows_of(mine), :] = stage[mine]

    for s in range(steps):
        before = None
        for r in range(rounds):
            forward, backward = orders(plan_ref[s * rounds + r:s * rounds + r + 1, :])
            if r == 0:
                moves[s, r] = forward
                moves_t[s, r] = backward
            else:
                moves[s, r] = dot(before[1], forward).astype(BF16)
                moves_t[s, r] = dot(backward, before[0]).astype(BF16)
            before = forward, backward
        moves[s, rounds] = before[1]

    for copy in incoming:
        copy.wait()

    x = held[...]
    for s in range(steps):
        gram = exact_dot(x.T, x)
        if groups > 1:
            grams[s, group] = gram
            shared = []
            for g in range(1, groups):
                copy = pltpu.make_async_remote_copy(
                    grams.at[s, group], grams.at[s, group], gram_send.at[s, g], gram_recv.at[s, g],
                    device_id=at(0, 0, g), device_id_type=MESH)
                copy.start()
                shared.append(copy)
            for copy in shared:
                copy.wait()
            gram = grams[s, 0]
            for g in range(1, groups):
                gram = gram + grams[s, g]
        rotation = diagonalizer(gram, s, moves, moves_t, rounds)
        if s + 1 < steps:
            bottoms[s] = exact_dot(x, rotation[:, half:])
            copy = pltpu.make_async_remote_copy(
                bottoms.at[s], landed.at[s], mid_sem.at[s, 0], mid_sem.at[s, 1],
                device_id=(me, right), device_id_type=MESH)
            copy.start()
            top = exact_dot(x, rotation[:, :half])
            copy.wait()
            x = jnp.concatenate([top, landed[s]], axis=1)

    ybot[...] = exact_dot(x, rotation[:, half:])
    outgoing = []
    for d in range(owners):
        copy = pltpu.make_async_remote_copy(
            ybot.at[rows_of((mine + d) % owners), :], arrived.at[1, mine], low_send.at[d], low_recv.at[d],
            device_id=at(d, 1), device_id_type=MESH)
        copy.start()
        outgoing.append(copy)
    ytop[...] = exact_dot(x, rotation[:, :half])
    for d in range(1, owners):
        copy = pltpu.make_async_remote_copy(
            ytop.at[rows_of((mine + d) % owners), :], arrived.at[0, mine], top_send.at[d], top_recv.at[d],
            device_id=at(d), device_id_type=MESH)
        copy.start()
        outgoing.append(copy)
    arrived[0, mine] = ytop[rows_of(mine), :]
    for copy in outgoing:
        copy.wait()
    for k in range(owners):
        for h in range(2):
            out_ref[pl.ds(2 * k + h, rows_here, stride=2 * owners), :] = arrived[h, k]


def body(mesh_sizes, matrix, plan):
    rows_here, pair_here, halves, half = matrix.shape
    steps, rounds, width = plan.shape
    rows, cols = mesh_sizes
    owners, groups = pair_here, rows // pair_here
    assert rows % pair_here == 0 and halves == 2 and cols > 1
    sizes = (owners, groups, cols, rows_here, steps, rounds, width)
    dma = pltpu.SemaphoreType.DMA
    rows_all = owners * rows_here
    vmem = pl.BlockSpec(memory_space=pltpu.VMEM)
    out = pl.pallas_call(
        functools.partial(kernel, sizes),
        out_shape=jax.ShapeDtypeStruct((rows_here * pair_here * 2, half), F32),
        in_specs=[vmem, vmem],
        out_specs=vmem,
        scratch_shapes=[
            pltpu.VMEM((owners, rows_here, width), F32),
            pltpu.VMEM((rows_all, width), F32),
            pltpu.VMEM((steps - 1, rows_all, half), F32),
            pltpu.VMEM((steps - 1, rows_all, half), F32),
            pltpu.VMEM((rows_all, half), F32),
            pltpu.VMEM((rows_all, half), F32),
            pltpu.VMEM((2, owners, rows_here, half), F32),
            pltpu.VMEM((steps, rounds + 1, width, width), BF16),
            pltpu.VMEM((steps, rounds, width, width), BF16),
            pltpu.VMEM((steps, groups, width, width) if groups > 1 else (1, 1, 8, 128), F32),
            dma((owners,)), dma((owners,)), dma((steps, 2)), dma((steps, groups)), dma((steps, groups)),
            dma((owners,)), dma((owners,)), dma((owners,)), dma((owners,)),
        ],
        compiler_params=pltpu.CompilerParams(collective_id=0, has_side_effects=True, vmem_limit_bytes=48 << 20),
    )(matrix.reshape(rows_here * pair_here * 2, half), plan.reshape(steps * rounds, width))
    return out.reshape(matrix.shape)


def solution(mesh):
    in_specs = (P("rows", "cols", None, None), P())
    out_specs = P("rows", "cols", None, None)
    sizes = (mesh.shape["rows"], mesh.shape["cols"])
    return jax.shard_map(functools.partial(body, sizes), mesh=mesh, in_specs=in_specs, out_specs=out_specs, check_vma=False)
```

time: 467 us -> 47.3 us (0.10)
  waiting for transfers between devices: 171 us -> 0 us
  local copies, waits for them, and re-layouts: 165 us -> 2.54 us
  matrix products: 92.9 us -> 0 us
  Pallas kernels: 0 us -> 44.5 us
  other arithmetic: 18 us -> 0 us
  between operations: 14.6 us -> 0.01 us
    psum x2 -> x0, waiting for transfers between devices: 162 us -> none  [the longest x1 92 us: full_grams(): return lax.psum(local_sum, 'rows')]
    dot_general x6 -> x0, local copies, waits for them, and re-layouts: 98.9 us -> none  [diagonalize(): jnp.einsum('pji,pjk->pik', rot_now, product, precision=lax.Precision.HIGH...]
    dot_general x34 -> x0, matrix products: 92.9 us -> none  [the longest x7 31.7 us: diagonalize(): jnp.einsum('pij,pjk->pik', grams, rot_now, precision=lax.Precision.HIGHEST)]
    pallas_call x0 -> x1, Pallas kernels: none -> 44.5 us  [body(): pl.pallas_call(functools.partial(kernel, sizes), out_shape=jax.ShapeDtype...]
    gather x16 -> x0, local copies, waits for them, and re-layouts: 21 us -> none  [diagonalize(): diagonal_now = jnp.diagonal(grams, axis1=1, axis2=2)]
    psum x1 -> x0, local copies, waits for them, and re-layouts: 17.5 us -> none  [full_grams(): return lax.psum(local_sum, 'rows')]
    concatenate x1 -> x0, local copies, waits for them, and re-layouts: 16.7 us -> none  [body(): grams = jnp.concatenate([upper_rows, lower_rows], axis=1)]
    convert_element_type x15 -> x0, other arithmetic: 9.61 us -> none  [diagonalize(): onehot = (partner[:, None] == indices[None, :]).astype(jnp.float32)]
  transfers between devices with their start and end apart: 5 -> 0, of which waited for: 4 -> 0; matrix products, arithmetic and copies ran while one was open for 4% -> 0% of each run, Pallas kernels for 0% -> 0%
where the time goes in v1:
time: 47.3 us; the launch traced here: 47.1 us
  Pallas kernels  44.5 us (94%)
  local copies, waits for them, and re-layouts  2.54 us (5%)
    pallas_call x1, Pallas kernels, body(): pl.pallas_call(functools.partial(kernel, sizes), out_shape=jax.ShapeDtype...  44.5 us
    unnamed x3, local copies, waits for them, and re-layouts  1.84 us

profile of v1, /device:TPU:0, one launch (start us, length us, event | category | flops | bytes accessed | tf_op | source)
XLA Modules:
  0.0 47.1 jit_solution(1865688667613955511)
XLA Ops:
  0.0 0.7 %reshape.10.plan_ref = s32[8,256]{1,0:T(8,128)S(1)} reshape(s32[2,4,256]{2,1,0:T(4,128)} %param.3) | data formatting | bytes 16384 | tf_op jit(solution)/shard_map/reshape | solution.py:245
  0.7 0.0 copy-start
  0.7 1.0 %copy-done = f32[64,8,2,128]{3,2,1,0:T(2,128)S(1)} copy-done((f32[64,8,2,128]{3,2,1,0:T(2,128)S(1)}, f32[64,8,2,128]{3,2,1,0:T(2,128)}, u32[]{:S(2)}) %copy-start) | copy-done | bytes 524312
  1.7 44.5 %shard_map.28 = f32[1024,128]{1,0:T(8,128)S(1)} custom-call(f32[1024,128]{1,0:T(8,128)S(1)} %bitcast.3, s32[8,256]{1,0:T(8,128)S(1)} %reshape.10.plan_ref), custom_call_target="tpu_custom_call" | custom-call | tf_op jit(solution)/shard_map/pallas_call | solution.py:225
  46.3 0.8 %copy.4 = f32[64,8,2,128]{3,2,1,0:T(2,128)} copy(f32[64,8,2,128]{3,2,1,0:T(2,128)S(1)} %bitcast.2) | data formatting | bytes 1048576
Async XLA Ops:
  0.7 1.0 %copy-start = (f32[64,8,2,128]{3,2,1,0:T(2,128)S(1)}, f32[64,8,2,128]{3,2,1,0:T(2,128)}, u32[]{:S(2)}) copy-start(f32[64,8,2,128]{3,2,1,0:T(2,128)} %param.2) | copy-start | bytes 1572868

commit v2 on v1

--- a/solution.py
+++ b/solution.py
@@ -91,29 +91,46 @@
     return forward, backward
 
 
-def diagonalizer(gram, step, moves, moves_t, rounds):
+def diagonalizer(gram, step, moves, moves_t, rounds, want_rotation):
     rotation = None
-    cosine = sine = None
+    cosines, sines = [], []
     for r in range(rounds):
         move = moves[step, r]
         if r == 0:
             turned = moved_transposed(gram, moves_t[step, r])
             gram = moved_columns(turned, move)
-            rotation = move.astype(F32)
         else:
-            turned = moved_transposed(rotated_columns(gram, cosine, sine), moves_t[step, r])
-            gram = moved_columns(rotated_columns(turned, cosine, sine), move)
-            rotation = moved_columns(rotation, move)
+            turned = moved_transposed(rotated_columns(gram, cosines[-1], sines[-1]), moves_t[step, r])
+            gram = moved_columns(rotated_columns(turned, cosines[-1], sines[-1]), move)
         cosine, sine = angles(gram)
-        rotation = rotated_columns(rotation, cosine, sine)
-    return moved_columns(rotation, moves[step, rounds])
-
-
-def kernel(sizes, x_ref, plan_ref, out_ref, stage, held, bottoms, landed, ytop, ybot, arrived, moves, moves_t, grams,
-           in_send, in_recv, mid_sem, gram_send, gram_recv, top_send, top_recv, low_send, low_recv):
+        cosines.append(cosine)
+        sines.append(sine)
+        if want_rotation:
+            rotation = move.astype(F32) if r == 0 else moved_columns(rotation, move)
+            rotation = rotated_columns(rotation, cosine, sine)
+    if want_rotation:
+        rotation = moved_columns(rotation, moves[step, rounds])
+    return jnp.concatenate(cosines + sines, axis=0), rotation
+
+
+def turn_rows(x, turns, step, moves, rounds):
+    pairs, rows, width = x.shape
+    half = width // 2
+    x = x.reshape(pairs * rows, width)
+    for r in range(rounds):
+        x = moved_columns(x, moves[step, r]).reshape(pairs, rows, width)
+        cosine, sine = turns[:, r:r + 1, :], turns[:, rounds + r:rounds + r + 1, :]
+        left, right = x[:, :, :half], x[:, :, half:]
+        x = jnp.concatenate([cosine * left - sine * right, sine * left + cosine * right], axis=2)
+        x = x.reshape(pairs * rows, width)
+    return moved_columns(x, moves[step, rounds]).reshape(pairs, rows, width)
+
+
+def kernel(sizes, x_ref, plan_ref, out_ref, stage, held, bottoms, landed, row_tops, row_low, row_landed, turns,
+           moves, moves_t, grams, in_send, in_recv, mid_sem, gram_send, gram_recv, turn_send, turn_recv,
+           row_send, row_recv):
     owners, groups, cols, rows_here, steps, rounds, width = sizes
     half = width // 2
-    rows_all = owners * rows_here
     me = lax.axis_index("rows")
     col = lax.axis_index("cols")
     group, mine = me // owners, me % owners
@@ -123,7 +140,7 @@
         row = ((group + group_shift) % groups) * owners + (mine + owner_shift) % owners
         return row, (col + col_shift) % cols
 
-    peers = {(o, c, 0) for o in range(owners) for c in (0, 1, cols - 1)} | {(0, 0, g) for g in range(groups)}
+    peers = {(o, 0, 0) for o in range(owners)} | {(0, c, 0) for c in (1, cols - 1)} | {(0, 0, g) for g in range(groups)}
     peers = sorted(peers - {(0, 0, 0)})
     barrier = pltpu.get_barrier_semaphore()
     for peer in peers:
@@ -148,7 +165,7 @@
     for s in range(steps):
         before = None
         for r in range(rounds):
-            forward, backward = orders(plan_ref[s * rounds + r:s * rounds + r + 1, :])
+            forward, backward = orders(plan_ref[s, r:r + 1, :])
             if r == 0:
                 moves[s, r] = forward
                 moves_t[s, r] = backward
@@ -162,6 +179,8 @@
         copy.wait()
 
     x = held[...]
+    chunks = 2 if owners % 2 == 0 else 1
+    passing = []
     for s in range(steps):
         gram = exact_dot(x.T, x)
         if groups > 1:
@@ -178,38 +197,56 @@
             gram = grams[s, 0]
             for g in range(1, groups):
                 gram = gram + grams[s, g]
-        rotation = diagonalizer(gram, s, moves, moves_t, rounds)
-        if s + 1 < steps:
+        last = s + 1 == steps
+        angle, rotation = diagonalizer(gram, s, moves, moves_t, rounds, not last)
+        turns[s, mine] = angle
+        told = []
+        for d in range(1, owners):
+            copy = pltpu.make_async_remote_copy(
+                turns.at[s, mine], turns.at[s, mine], turn_send.at[s, d], turn_recv.at[s, d],
+                device_id=at(d), device_id_type=MESH)
+            copy.start()
+            told.append(copy)
+        if not last:
             bottoms[s] = exact_dot(x, rotation[:, half:])
-            copy = pltpu.make_async_remote_copy(
+            crossing = pltpu.make_async_remote_copy(
                 bottoms.at[s], landed.at[s], mid_sem.at[s, 0], mid_sem.at[s, 1],
                 device_id=(me, right), device_id_type=MESH)
+            crossing.start()
+            top = exact_dot(x, rotation[:, :half])
+        if s > 0:
+            for copy in passing:
+                copy.wait()
+        for copy in told:
+            copy.wait()
+        passing = []
+        size = owners // chunks
+        for q in range(chunks):
+            part = slice(q * size, (q + 1) * size)
+            if s == 0:
+                rows = stage[part]
+            else:
+                rows = jnp.concatenate([row_tops[s - 1, part], row_landed[s - 1, part]], axis=2)
+            rows = turn_rows(rows, turns[s, part], s, moves, rounds)
+            row_low[s, part] = rows[:, :, half:]
+            copy = pltpu.make_async_remote_copy(
+                row_low.at[s, part], row_landed.at[s, part], row_send.at[s, q], row_recv.at[s, q],
+                device_id=(me, right), device_id_type=MESH)
             copy.start()
-            top = exact_dot(x, rotation[:, :half])
-            copy.wait()
+            passing.append(copy)
+            if last:
+                for k in range(size):
+                    out_ref[pl.ds(2 * (q * size + k), rows_here, stride=2 * owners), :] = rows[k, :, :half]
+            else:
+                row_tops[s, part] = rows[:, :, :half]
+        if not last:
+            crossing.wait()
             x = jnp.concatenate([top, landed[s]], axis=1)
 
-    ybot[...] = exact_dot(x, rotation[:, half:])
-    outgoing = []
-    for d in range(owners):
-        copy = pltpu.make_async_remote_copy(
-            ybot.at[rows_of((mine + d) % owners), :], arrived.at[1, mine], low_send.at[d], low_recv.at[d],
-            device_id=at(d, 1), device_id_type=MESH)
-        copy.start()
-        outgoing.append(copy)
-    ytop[...] = exact_dot(x, rotation[:, :half])
-    for d in range(1, owners):
-        copy = pltpu.make_async_remote_copy(
-            ytop.at[rows_of((mine + d) % owners), :], arrived.at[0, mine], top_send.at[d], top_recv.at[d],
-            device_id=at(d), device_id_type=MESH)
-        copy.start()
-        outgoing.append(copy)
-    arrived[0, mine] = ytop[rows_of(mine), :]
-    for copy in outgoing:
-        copy.wait()
-    for k in range(owners):
-        for h in range(2):
-            out_ref[pl.ds(2 * k + h, rows_here, stride=2 * owners), :] = arrived[h, k]
+    for q in range(chunks):
+        passing[q].wait()
+        for k in range(q * size, (q + 1) * size):
+            out_ref[pl.ds(2 * k + 1, rows_here, stride=2 * owners), :] = row_landed[steps - 1, k]
 
 
 def body(mesh_sizes, matrix, plan):
@@ -232,17 +269,18 @@
             pltpu.VMEM((rows_all, width), F32),
             pltpu.VMEM((steps - 1, rows_all, half), F32),
             pltpu.VMEM((steps - 1, rows_all, half), F32),
-            pltpu.VMEM((rows_all, half), F32),
-            pltpu.VMEM((rows_all, half), F32),
-            pltpu.VMEM((2, owners, rows_here, half), F32),
+            pltpu.VMEM((steps, owners, rows_here, half), F32),
+            pltpu.VMEM((steps, owners, rows_here, half), F32),
+            pltpu.VMEM((steps, owners, rows_here, half), F32),
+            pltpu.VMEM((steps, owners, 2 * rounds, half), F32),
             pltpu.VMEM((steps, rounds + 1, width, width), BF16),
             pltpu.VMEM((steps, rounds, width, width), BF16),
             pltpu.VMEM((steps, groups, width, width) if groups > 1 else (1, 1, 8, 128), F32),
             dma((owners,)), dma((owners,)), dma((steps, 2)), dma((steps, groups)), dma((steps, groups)),
-            dma((owners,)), dma((owners,)), dma((owners,)), dma((owners,)),
+            dma((steps, owners)), dma((steps, owners)), dma((steps, 2)), dma((steps, 2)),
         ],
         compiler_params=pltpu.CompilerParams(collective_id=0, has_side_effects=True, vmem_limit_bytes=48 << 20),
-    )(matrix.reshape(rows_here * pair_here * 2, half), plan.reshape(steps * rounds, width))
+    )(matrix.reshape(rows_here * pair_here * 2, half), plan)
     return out.reshape(matrix.shape)
 
 

time: 47.3 us -> 45.4 us (0.960)
  Pallas kernels: 44.5 us -> 42.6 us
    pallas_call x1, Pallas kernels: 44.5 us -> 42.6 us  [body(): pl.pallas_call(functools.partial(kernel, sizes), out_shape=jax.ShapeDtype...]
    reshape x1 -> x0, local copies, waits for them, and re-layouts: 0.7 us -> none  [body(): plan.reshape(steps * rounds, width)]
    unnamed x3 -> x5, local copies, waits for them, and re-layouts: 1.84 us -> 2.53 us
where the time goes in v2:
time: 45.4 us; the launch traced here: 45.2 us
  Pallas kernels  42.6 us (94%)
  local copies, waits for them, and re-layouts  2.53 us (6%)
    pallas_call x1, Pallas kernels, body(): pl.pallas_call(functools.partial(kernel, sizes), out_shape=jax.ShapeDtype...  42.6 us
    unnamed x5, local copies, waits for them, and re-layouts  2.53 us

profile of v2, /device:TPU:0, one launch (start us, length us, event | category | flops | bytes accessed | tf_op | source)
XLA Modules:
  0.0 45.2 jit_solution(8777747673305701410)
XLA Ops:
  0.0 0.0 copy-start
  0.0 1.0 %copy-done = f32[64,8,2,128]{3,2,1,0:T(2,128)S(1)} copy-done((f32[64,8,2,128]{3,2,1,0:T(2,128)S(1)}, f32[64,8,2,128]{3,2,1,0:T(2,128)}, u32[]{:S(2)}) %copy-start) | copy-done | bytes 524312
  1.0 0.0 copy-start.1
  1.0 0.7 %copy-done.1 = s32[2,4,256]{2,1,0:T(4,128)S(1)} copy-done((s32[2,4,256]{2,1,0:T(4,128)S(1)}, s32[2,4,256]{2,1,0:T(4,128)}, u32[]{:S(2)}) %copy-start.1) | copy-done | bytes 8216
  1.7 42.6 %shard_map.28 = f32[1024,128]{1,0:T(8,128)S(1)} custom-call(f32[1024,128]{1,0:T(8,128)S(1)} %bitcast.3, s32[2,4,256]{2,1,0:T(4,128)S(1)} %copy-done.1), custom_call_target="tpu_custom_call" | custom-call | tf_op jit(solution)/shard_map/pallas_call | solution.py:262
  44.4 0.8 %copy.4 = f32[64,8,2,128]{3,2,1,0:T(2,128)} copy(f32[64,8,2,128]{3,2,1,0:T(2,128)S(1)} %bitcast.2) | data formatting | bytes 1048576
Async XLA Ops:
  0.0 1.0 %copy-start = (f32[64,8,2,128]{3,2,1,0:T(2,128)S(1)}, f32[64,8,2,128]{3,2,1,0:T(2,128)}, u32[]{:S(2)}) copy-start(f32[64,8,2,128]{3,2,1,0:T(2,128)} %param.2) | copy-start | bytes 1572868
  1.0 0.7 %copy-start.1 = (s32[2,4,256]{2,1,0:T(4,128)S(1)}, s32[2,4,256]{2,1,0:T(4,128)}, u32[]{:S(2)}) copy-start(s32[2,4,256]{2,1,0:T(4,128)} %plan_ref.1) | copy-start | bytes 24580

commit v3 on v2

--- a/solution.py
+++ b/solution.py
@@ -154,7 +154,7 @@
         return pl.ds(pl.multiple_of(owner * rows_here, rows_here), rows_here)
 
     incoming = []
-    for d in range(1, owners):
+    for d in sorted(range(1, owners), key=lambda d: -min(d, owners - d)):
         copy = pltpu.make_async_remote_copy(
             stage.at[(mine + d) % owners], held.at[rows_of(mine), :], in_send.at[d], in_recv.at[d],
             device_id=at(d), device_id_type=MESH)

time: 45.4 us -> 45.4 us (level)
  no operation moved by 1% of the time
where the time goes in v3:
time: 45.4 us; the launch traced here: 45.2 us
  Pallas kernels  42.6 us (94%)
  local copies, waits for them, and re-layouts  2.53 us (6%)
    pallas_call x1, Pallas kernels, body(): pl.pallas_call(functools.partial(kernel, sizes), out_shape=jax.ShapeDtype...  42.6 us
    unnamed x5, local copies, waits for them, and re-layouts  2.53 us

profile of v3, /device:TPU:0, one launch (start us, length us, event | category | flops | bytes accessed | tf_op | source)
XLA Modules:
  0.0 45.2 jit_solution(15742595276631581923)
XLA Ops:
  0.0 0.0 copy-start
  0.0 1.0 %copy-done = f32[64,8,2,128]{3,2,1,0:T(2,128)S(1)} copy-done((f32[64,8,2,128]{3,2,1,0:T(2,128)S(1)}, f32[64,8,2,128]{3,2,1,0:T(2,128)}, u32[]{:S(2)}) %copy-start) | copy-done | bytes 524312
  1.0 0.0 copy-start.1
  1.0 0.7 %copy-done.1 = s32[2,4,256]{2,1,0:T(4,128)S(1)} copy-done((s32[2,4,256]{2,1,0:T(4,128)S(1)}, s32[2,4,256]{2,1,0:T(4,128)}, u32[]{:S(2)}) %copy-start.1) | copy-done | bytes 8216
  1.7 42.6 %shard_map.28 = f32[1024,128]{1,0:T(8,128)S(1)} custom-call(f32[1024,128]{1,0:T(8,128)S(1)} %bitcast.3, s32[2,4,256]{2,1,0:T(4,128)S(1)} %copy-done.1), custom_call_target="tpu_custom_call" | custom-call | tf_op jit(solution)/shard_map/pallas_call | solution.py:262
  44.4 0.8 %copy.4 = f32[64,8,2,128]{3,2,1,0:T(2,128)} copy(f32[64,8,2,128]{3,2,1,0:T(2,128)S(1)} %bitcast.2) | data formatting | bytes 1048576
Async XLA Ops:
  0.0 1.0 %copy-start = (f32[64,8,2,128]{3,2,1,0:T(2,128)S(1)}, f32[64,8,2,128]{3,2,1,0:T(2,128)}, u32[]{:S(2)}) copy-start(f32[64,8,2,128]{3,2,1,0:T(2,128)} %param.2) | copy-start | bytes 1572868
  1.0 0.7 %copy-start.1 = (s32[2,4,256]{2,1,0:T(4,128)S(1)}, s32[2,4,256]{2,1,0:T(4,128)}, u32[]{:S(2)}) copy-start(s32[2,4,256]{2,1,0:T(4,128)} %plan_ref.1) | copy-start | bytes 24580

commit v4 on v2

--- a/solution.py
+++ b/solution.py
@@ -116,9 +116,9 @@
 def turn_rows(x, turns, step, moves, rounds):
     pairs, rows, width = x.shape
     half = width // 2
-    x = x.reshape(pairs * rows, width)
     for r in range(rounds):
-        x = moved_columns(x, moves[step, r]).reshape(pairs, rows, width)
+        if r > 0:
+            x = moved_columns(x, moves[step, r]).reshape(pairs, rows, width)
         cosine, sine = turns[:, r:r + 1, :], turns[:, rounds + r:rounds + r + 1, :]
         left, right = x[:, :, :half], x[:, :, half:]
         x = jnp.concatenate([cosine * left - sine * right, sine * left + cosine * right], axis=2)
@@ -217,17 +217,22 @@
         if s > 0:
             for copy in passing:
                 copy.wait()
-        for copy in told:
-            copy.wait()
-        passing = []
         size = owners // chunks
+        ordered = []
         for q in range(chunks):
             part = slice(q * size, (q + 1) * size)
             if s == 0:
                 rows = stage[part]
             else:
                 rows = jnp.concatenate([row_tops[s - 1, part], row_landed[s - 1, part]], axis=2)
-            rows = turn_rows(rows, turns[s, part], s, moves, rounds)
+            flat = moved_columns(rows.reshape(size * rows_here, width), moves[s, 0])
+            ordered.append(flat.reshape(size, rows_here, width))
+        for copy in told:
+            copy.wait()
+        passing = []
+        for q in range(chunks):
+            part = slice(q * size, (q + 1) * size)
+            rows = turn_rows(ordered[q], turns[s, part], s, moves, rounds)
             row_low[s, part] = rows[:, :, half:]
             copy = pltpu.make_async_remote_copy(
                 row_low.at[s, part], row_landed.at[s, part], row_send.at[s, q], row_recv.at[s, q],

time: 45.4 us -> 44.5 us (0.980)
  Pallas kernels: 42.6 us -> 41.8 us
    pallas_call x1, Pallas kernels: 42.6 us -> 41.8 us  [body(): pl.pallas_call(functools.partial(kernel, sizes), out_shape=jax.ShapeDtype...]
where the time goes in v4:
time: 44.5 us; the launch traced here: 44.3 us
  Pallas kernels  41.8 us (94%)
  local copies, waits for them, and re-layouts  2.53 us (6%)
    pallas_call x1, Pallas kernels, body(): pl.pallas_call(functools.partial(kernel, sizes), out_shape=jax.ShapeDtype...  41.8 us
    unnamed x5, local copies, waits for them, and re-layouts  2.53 us

profile of v4, /device:TPU:0, one launch (start us, length us, event | category | flops | bytes accessed | tf_op | source)
XLA Modules:
  0.0 44.3 jit_solution(1780508884633841777)
XLA Ops:
  0.0 0.0 copy-start
  0.0 1.0 %copy-done = f32[64,8,2,128]{3,2,1,0:T(2,128)S(1)} copy-done((f32[64,8,2,128]{3,2,1,0:T(2,128)S(1)}, f32[64,8,2,128]{3,2,1,0:T(2,128)}, u32[]{:S(2)}) %copy-start) | copy-done | bytes 524312
  1.0 0.0 copy-start.1
  1.0 0.7 %copy-done.1 = s32[2,4,256]{2,1,0:T(4,128)S(1)} copy-done((s32[2,4,256]{2,1,0:T(4,128)S(1)}, s32[2,4,256]{2,1,0:T(4,128)}, u32[]{:S(2)}) %copy-start.1) | copy-done | bytes 8216
  1.7 41.8 %shard_map.28 = f32[1024,128]{1,0:T(8,128)S(1)} custom-call(f32[1024,128]{1,0:T(8,128)S(1)} %bitcast.3, s32[2,4,256]{2,1,0:T(4,128)S(1)} %copy-done.1), custom_call_target="tpu_custom_call" | custom-call | tf_op jit(solution)/shard_map/pallas_call | solution.py:267
  43.5 0.8 %copy.4 = f32[64,8,2,128]{3,2,1,0:T(2,128)} copy(f32[64,8,2,128]{3,2,1,0:T(2,128)S(1)} %bitcast.2) | data formatting | bytes 1048576
Async XLA Ops:
  0.0 1.0 %copy-start = (f32[64,8,2,128]{3,2,1,0:T(2,128)S(1)}, f32[64,8,2,128]{3,2,1,0:T(2,128)}, u32[]{:S(2)}) copy-start(f32[64,8,2,128]{3,2,1,0:T(2,128)} %param.2) | copy-start | bytes 1572868
  1.0 0.7 %copy-start.1 = (s32[2,4,256]{2,1,0:T(4,128)S(1)}, s32[2,4,256]{2,1,0:T(4,128)}, u32[]{:S(2)}) copy-start(s32[2,4,256]{2,1,0:T(4,128)} %plan_ref.1) | copy-start | bytes 24580
